TPU v7x, 32 devices: a whole 2x2x4 slice. The times are simulated.
32 devices in a mesh: pop: 8 (over y, x, core), tile: 4 (over z).
Axes of the slice: x: 2, y: 2, z: 4, core: 2. Of those that a mesh axis runs over, the one named last changes fastest.
Arguments:
- weights: int32 [8, 8], replicated, may hold values from -2 to 3
- terminal: float32 [8, 32, 2048], P('pop', 'tile'), may hold values from -4.5 to 4.5
- density_history: bfloat16 [8, 8, 32, 2048], P('pop', None, 'tile'), may hold values from 0.19921875 to 2
- density_init: float32 [8, 32, 2048], P('pop', 'tile'), may hold values from 0.2 to 2
Outputs:
- values: float32 [8, 8, 32, 2048], P('pop', None, 'tile')
- density_final: float32 [8, 32, 2048], P('pop', 'tile')
All inputs are finite; a program needn't handle non-finite values.
Results may differ from a plain program's by a relative error of at most 0.0003.
Values may be sent and summed in bfloat16 or wider, within the bound.
A program may use at most 64 MiB of HBM per device.

v0:
```python
import functools

import jax
import jax.numpy as jnp
from jax import lax
from jax.experimental import pallas as pl
from jax.experimental.pallas import tpu as pltpu
from jax.sharding import PartitionSpec as P

time_step = 0.2
viscosity = 0.2
LANES = 128
WINDOWS = 4
SPAN = LANES // WINDOWS
LAG_B, LAG_C, LAG_D = 3, 3, 4
DIRECT = 10


def kernel(pops, tiles, weights, terminal_in, history_in, initial_in, values, density_out,
           terminal, history, initial, load_sem, gathered, gathered_rim, start_value, start_mass, start_rim,
           rim_send, rim_send_f32, swept, mass_main, slope_r, slope_c, sums_own, sums_all,
           tile_send, tile_recv, tile_self, first_send, first_recv, first_self,
           x_send, x_recv, y_send, y_recv, half_a_send, half_a_recv, half_b_send, half_b_recv,
           core_send, core_recv, back_send, back_recv, back_self):
    steps, rows, cols = history.shape
    width = cols // tiles
    groups = steps // WINDOWS
    total_rows = tiles * rows
    outer = pops // 4
    half = tiles // 2
    me = lax.axis_index("tile")
    own = lax.axis_index("pop")
    core = own % 2
    plane = (own // 2) % 2
    line = own // 4

    def pop_of(a, b, c):
        return (a * 2 + b) * 2 + c

    partner = pop_of(line, plane, 1 - core)
    across = pop_of(line, 1 - plane, core)
    lines = [(line + j) % outer for j in range(1, outer)]
    columns = [pop_of(a, plane, core) for a in lines]
    diagonal = [pop_of(a, 1 - plane, core) for a in lines]
    peers = [(me + d) % tiles for d in range(1, tiles)]

    barrier = pltpu.get_barrier_semaphore()
    greeted = [{"tile": z} for z in peers] + [{"pop": q} for q in [partner, across] + columns + diagonal]
    for there in greeted:
        pl.semaphore_signal(barrier, inc=1, device_id=there, device_id_type=pl.DeviceIdType.MESH)

    loads = [pltpu.make_async_copy(src, dst, load_sem.at[n]) for n, (src, dst) in enumerate(
        [(terminal_in, terminal), (initial_in, initial), (history_in, history)])]
    for load in loads:
        load.start()
    for load in loads:
        load.wait()
    lane = lax.broadcasted_iota(jnp.int32, (rows, LANES), 1)
    window = ((lane + SPAN // 2) % LANES) // SPAN
    right_side = lane < LANES // 2

    def rim_of(block, z):
        right = ((z + 1) % tiles) * width
        left = ((z + tiles - 1) % tiles) * width + width - LANES
        return jnp.where(right_side, block[:, right:right + LANES], block[:, left:left + LANES])

    def packed(parts):
        out = parts[0]
        for k in range(1, len(parts)):
            out = jnp.where(window == k, pltpu.roll(parts[k], SPAN * k, 1), out)
        return out

    for z in range(tiles):
        rim_send_f32[z] = packed([rim_of(terminal[...], z), rim_of(initial[...], z)])
    for g in range(groups):
        for z in range(tiles):
            parts = [rim_of(history[steps - 1 - (g * WINDOWS + k)].astype(jnp.float32), z)
                     for k in range(WINDOWS)]
            rim_send[z, g] = packed(parts).astype(jnp.bfloat16)

    pl.semaphore_wait(barrier, len(greeted))

    def cut(z):
        return pl.ds(pl.multiple_of(z * width, LANES), width)

    sent = []

    def remote(src, dst, send, recv, there):
        copy = pltpu.make_async_remote_copy(src_ref=src, dst_ref=dst, send_sem=send, recv_sem=recv,
                                            device_id=there, device_id_type=pl.DeviceIdType.MESH)
        copy.start()
        return copy

    def arrived(ref, sem):
        pltpu.make_async_copy(ref, ref, sem).wait()

    firsts = [
        (lambda z: terminal.at[:, cut(z)], start_value),
        (lambda z: rim_send_f32.at[z], start_rim),
        (lambda z: initial.at[:, cut(z)], start_mass),
    ]

    def exchange_first(n):
        src, dst = firsts[n]
        pltpu.make_async_copy(src(me), dst.at[me], first_self.at[n]).start()
        for z in peers:
            remote(src(z), dst.at[me], first_send.at[n], first_recv.at[n], {"tile": z})

    def wait_first(n):
        dst = firsts[n][1]
        pltpu.make_async_copy(firsts[n][0](me), dst.at[me], first_self.at[n]).wait()
        arrived(dst.at[pl.ds(0, tiles - 1)], first_recv.at[n])
        arrived(dst.at[pl.ds(0, tiles - 1)], first_send.at[n])

    items = []
    for g in range(groups):
        items.append(("rim", g))
        for k in range(WINDOWS):
            items.append(("main", steps - 1 - (g * WINDOWS + k)))

    def block(n, q):
        kind, index = items[n]
        return gathered.at[q, index] if kind == "main" else gathered_rim.at[q, index]

    def piece(n, z):
        kind, index = items[n]
        return history.at[index, :, cut(z)] if kind == "main" else rim_send.at[z, index]

    def exchange_item(n):
        pltpu.make_async_copy(piece(n, me), block(n, own).at[me], tile_self.at[n]).start()
        for z in peers:
            remote(piece(n, z), block(n, own).at[me], tile_send.at[n], tile_recv.at[n], {"tile": z})

    exchange_item(0)
    exchange_item(1)
    exchange_first(0)
    exchange_first(1)
    for n in range(2, len(items)):
        exchange_item(n)
    exchange_first(2)

    def to_partner(n, kind, q):
        sent.append(remote(block(n, q), block(n, q), core_send.at[kind, n], core_recv.at[kind, n],
                           {"pop": partner}))

    def direct(n):
        return n >= len(items) - DIRECT

    def stage_a(n):
        pltpu.make_async_copy(piece(n, me), block(n, own).at[me], tile_self.at[n]).wait()
        arrived(block(n, own).at[pl.ds(0, tiles - 1)], tile_recv.at[n])
        mine = block(n, own)
        sent.append(remote(mine, mine, x_send.at[n], x_recv.at[n], {"pop": across}))
        for j, q in enumerate(columns):
            sent.append(remote(mine, mine, y_send.at[j, n], y_recv.at[j, n], {"pop": q}))
        if direct(n):
            for j, q in enumerate(diagonal):
                sent.append(remote(mine, mine, half_a_send.at[j, n], half_a_recv.at[j, n], {"pop": q}))
        to_partner(n, 0, own)

    def part(n, q, which):
        return block(n, q).at[pl.ds(which * half, half)]

    def stage_b(n):
        arrived(block(n, across), x_recv.at[n])
        ref = part(n, across, 1)
        for j, q in enumerate([] if direct(n) else columns):
            sent.append(remote(ref, ref, half_b_send.at[j, n], half_b_recv.at[j, n], {"pop": q}))
        to_partner(n, 1, across)
        for j in range(outer - 1):
            q = columns[outer - 2 - j]
            arrived(block(n, q), y_recv.at[j, n])
            ref = part(n, q, 0)
            if not direct(n):
                sent.append(remote(ref, ref, half_a_send.at[j, n], half_a_recv.at[j, n], {"pop": across}))
            to_partner(n, 2 + j, q)

    def stage_c(n):
        for j in range(outer - 1):
            q = diagonal[outer - 2 - j]
            if direct(n):
                arrived(block(n, q), half_a_recv.at[j, n])
            else:
                arrived(part(n, q, 0), half_a_recv.at[j, n])
                arrived(part(n, q, 1), half_b_recv.at[j, n])
            to_partner(n, 1 + outer + j, q)

    def other(q):
        return q + 1 - 2 * (q % 2)

    def coupled(n):
        for kind in range(2 * outer):
            if kind == 0:
                q = own
            elif kind == 1:
                q = across
            elif kind < 1 + outer:
                q = columns[outer - 2 - (kind - 2)]
            else:
                q = diagonal[outer - 2 - (kind - 1 - outer)]
            arrived(block(n, other(q)), core_recv.at[kind, n])
        total = None
        for q in range(pops):
            factor = weights[own, q].astype(jnp.float32) * (1.0 / pops)
            term = factor * block(n, q)[...].astype(jnp.float32)
            total = term if total is None else total + term
        return total.reshape(total_rows, total.shape[-1])

    full = width + LANES

    def ahead_r(x):
        return pltpu.roll(x, total_rows - 1, 0)

    def behind_r(x):
        return pltpu.roll(x, 1, 0)

    def ahead_c(x):
        return pltpu.roll(x, full - 1, 1)

    def behind_c(x):
        return pltpu.roll(x, 1, 1)

    def rim_at(rim, k):
        return rim if k == 0 else pltpu.roll(rim, LANES - SPAN * k, 1)

    def send_back(src, dst, n):
        pltpu.make_async_copy(src.at[me], dst.at[:, cut(me)], back_self.at[n]).start()
        for z in peers:
            remote(src.at[z], dst.at[:, cut(me)], back_send.at[n], back_recv.at[n], {"tile": z})

    def wait_back(src, dst, n):
        pltpu.make_async_copy(src.at[me], dst.at[:, cut(me)], back_self.at[n]).wait()
        landed = dst.at[:, pl.ds(0, (tiles - 1) * width)]
        arrived(landed, back_recv.at[n])
        arrived(landed, back_send.at[n])

    state = {}

    def stage_d(n):
        kind, t = items[n]
        if n == 0:
            for m in range(2):
                wait_first(m)
            main = start_value[...].reshape(total_rows, width)
            state["u"] = jnp.concatenate([main, start_rim[...].reshape(total_rows, LANES)], axis=1)
        if kind == "rim":
            state["rim"] = coupled(n)
            return
        k = (steps - 1 - t) % WINDOWS
        source = jnp.concatenate([coupled(n), rim_at(state["rim"], k)], axis=1)
        u = state["u"]
        dr = ahead_r(u) - u
        dc = ahead_c(u) - u
        if t + 1 < steps:
            slope_r[t + 1] = dr
            slope_c[t + 1] = dc
        er, ec = behind_r(dr), behind_c(dc)
        br, bc = jnp.maximum(er, 0.0), jnp.maximum(ec, 0.0)
        ar, ac = jnp.minimum(dr, 0.0), jnp.minimum(dc, 0.0)
        lap = (dr - er) + (dc - ec)
        ham = 0.5 * ((br * br + ar * ar) + (bc * bc + ac * ac))
        u = u + time_step * (viscosity * lap - ham + source)
        state["u"] = u
        main = u[:, :width]
        swept[t] = main.reshape(tiles, rows, width)
        send_back(swept.at[t], values.at[t], t)
        line_sum = jnp.sum(main, axis=0, keepdims=True)
        folded = line_sum[:, :LANES]
        for j in range(1, width // LANES):
            folded = folded + line_sum[:, j * LANES:(j + 1) * LANES]
        sums_own[t:t + 1, :] = folded

    count = len(items)
    for i in range(count + LAG_D):
        if i < count:
            stage_a(i)
        if 0 <= i - LAG_B < count:
            stage_b(i - LAG_B)
        if 0 <= i - LAG_C < count:
            stage_c(i - LAG_C)
        if 0 <= i - LAG_D < count:
            stage_d(i - LAG_D)

    sums_n = steps + 1
    sums_all[me] = sums_own[...]
    for z in peers:
        remote(sums_own, sums_all.at[me], back_send.at[sums_n], back_recv.at[sums_n], {"tile": z})

    wait_first(2)
    u = state["u"]
    mass = jnp.concatenate([start_mass[...].reshape(total_rows, width),
                            rim_at(start_rim[...].reshape(total_rows, LANES), 1)], axis=1)
    for t in range(steps):
        if t == 0:
            dr, dc = ahead_r(u) - u, ahead_c(u) - u
        else:
            dr, dc = slope_r[t], slope_c[t]
        mr, mc = ahead_r(mass), ahead_c(mass)
        flux_r = jnp.maximum(-dr, 0.0) * mass + jnp.minimum(-dr, 0.0) * mr
        flux_c = jnp.maximum(-dc, 0.0) * mass + jnp.minimum(-dc, 0.0) * mc
        net_r = viscosity * (mr - mass) - flux_r
        net_c = viscosity * (mc - mass) - flux_c
        mass = mass + time_step * ((net_r - behind_r(net_r)) + (net_c - behind_c(net_c)))
    mass_main[...] = mass[:, :width].reshape(tiles, rows, width)
    send_back(mass_main, density_out, steps)

    arrived(sums_all.at[pl.ds(0, tiles - 1)], back_recv.at[sums_n])
    arrived(sums_all.at[pl.ds(0, tiles - 1)], back_send.at[sums_n])
    grand = jnp.sum(jnp.sum(sums_all[...], axis=0), axis=1, keepdims=True) * (1.0 / (total_rows * cols))
    for t in reversed(range(steps)):
        wait_back(swept.at[t], values.at[t], t)
        values[t] = values[t] - grand[t:t + 1, :]
    wait_back(mass_main, density_out, steps)
    for n in range(count):
        arrived(block(n, own).at[pl.ds(0, tiles - 1)], tile_send.at[n])
    for copy in sent:
        copy.wait_send()


def finish(values, density, values_out, density_out, sems):
    copies = [
        pltpu.make_async_copy(values, values_out, sems.at[0]),
        pltpu.make_async_copy(density, density_out, sems.at[1]),
    ]
    for copy in copies:
        copy.start()
    for copy in copies:
        copy.wait()


def per_device(pops, tiles, weights, terminal, density_history, density_init):
    _, steps, rows, cols = density_history.shape
    width = cols // tiles
    groups = steps // WINDOWS
    items = steps + groups
    outer = pops // 4
    total_rows = tiles * rows
    full = width + LANES
    dma = pltpu.SemaphoreType.DMA
    lines = max(outer - 1, 1)
    vmem = pl.BlockSpec(memory_space=pltpu.VMEM)
    anywhere = pl.BlockSpec(memory_space=pl.ANY)
    values, density = pl.pallas_call(
        functools.partial(kernel, pops, tiles),
        out_shape=(
            pltpu.VMEM((steps, rows, cols), jnp.float32),
            pltpu.VMEM((rows, cols), jnp.float32),
        ),
        in_specs=[pl.BlockSpec(memory_space=pltpu.SMEM), anywhere, anywhere, anywhere],
        out_specs=(vmem, vmem),
        scratch_shapes=[
            pltpu.VMEM((rows, cols), jnp.float32),
            pltpu.VMEM((steps, rows, cols), jnp.bfloat16),
            pltpu.VMEM((rows, cols), jnp.float32),
            dma((3,)),
            pltpu.VMEM((pops, steps, tiles, rows, width), jnp.bfloat16),
            pltpu.VMEM((pops, groups, tiles, rows, LANES), jnp.bfloat16),
            pltpu.VMEM((tiles, rows, width), jnp.float32),
            pltpu.VMEM((tiles, rows, width), jnp.float32),
            pltpu.VMEM((tiles, rows, LANES), jnp.float32),
            pltpu.VMEM((tiles, groups, rows, LANES), jnp.bfloat16),
            pltpu.VMEM((tiles, rows, LANES), jnp.float32),
            pltpu.VMEM((steps, tiles, rows, width), jnp.float32),
            pltpu.VMEM((tiles, rows, width), jnp.float32),
            pltpu.VMEM((steps, total_rows, full), jnp.float32),
            pltpu.VMEM((steps, total_rows, full), jnp.float32),
            pltpu.VMEM((steps, LANES), jnp.float32),
            pltpu.VMEM((tiles, steps, LANES), jnp.float32),
            dma((items,)), dma((items,)), dma((items,)),
            dma((3,)), dma((3,)), dma((3,)),
            dma((items,)), dma((items,)),
            dma((lines, items)), dma((lines, items)),
            dma((lines, items)), dma((lines, items)),
            dma((lines, items)), dma((lines, items)),
            dma((2 * outer, items)), dma((2 * outer, items)),
            dma((steps + 2,)), dma((steps + 2,)), dma((steps + 1,)),
        ],
        compiler_params=pltpu.CompilerParams(collective_id=0, has_side_effects=True),
    )(weights, terminal[0], density_history[0], density_init[0])
    values, density = pl.pallas_call(
        finish,
        out_shape=(
            jax.ShapeDtypeStruct((steps, rows, cols), jnp.float32),
            jax.ShapeDtypeStruct((rows, cols), jnp.float32),
        ),
        in_specs=[anywhere, anywhere],
        out_specs=(anywhere, anywhere),
        scratch_shapes=[dma((2,))],
        compiler_params=pltpu.CompilerParams(vmem_limit_bytes=8 * 1024 * 1024),
    )(values, density)
    return values[None], density[None]


def solution(mesh):
    in_specs = (P(), P("pop", "tile", None), P("pop", None, "tile", None), P("pop", "tile", None))
    out_specs = (P("pop", None, "tile", None), P("pop", "tile", None))
    body = functools.partial(per_device, mesh.shape["pop"], mesh.shape["tile"])
    return jax.shard_map(body, mesh=mesh, in_specs=in_specs, out_specs=out_specs, check_vma=False)
```

profile of v0, /device:TPU:0, one launch (start us, length us, event | category | flops | bytes accessed | tf_op | source)
XLA Modules:
  0.0 36.6 jit_solution(947265643889522673)
XLA Ops:
  0.6 35.1 %shard_map.59 = (f32[8,8,2048]{2,1,0:T(8,128)S(1)}, f32[8,2048]{1,0:T(8,128)S(1)}) custom-call(s32[8,8]{1,0:T(8,128)} %weights.1, f32[8,2048]{1,0:T(8,128)} %bitcast.6, bf16[8,8,2048]{2,1,0:T(8,128)(2,1)} %bitcast.5, f32[8,2048]{1,0:T(8,128)} %bitcast.7), custom_call_target="tpu_custom_call" | custom-call | tf_op jit(solution)/shard_map/pallas_call | solution.py:343
  35.8 0.8 %shard_map.60 = (f32[8,8,2048]{2,1,0:T(8,128)}, f32[8,2048]{1,0:T(8,128)}) custom-call(f32[8,8,2048]{2,1,0:T(8,128)S(1)} %get-tuple-element.6.values, f32[8,2048]{1,0:T(8,128)S(1)} %get-tuple-element.7.density), custom_call_target="tpu_custom_call" | custom-call | tf_op jit(solution)/shard_map/pallas_call | solution.py:380
where the time goes:
time: 36.8 us; the launch traced here: 36.6 us
  Pallas kernels  35.9 us (98%)
  between operations  0.64 us (2%)
    pallas_call x1, Pallas kernels, per_device(): pl.pallas_call(functools.partial(kernel, pops, tiles), out_shape=(pltpu.V...  35.1 us
    pallas_call x1, Pallas kernels, per_device(): pl.pallas_call(finish, out_shape=(jax.ShapeDtypeStruct((steps, rows, cols...  0.82 us

commit v1 on v0

v1 whole, which is shorter than its diff:
```python
import functools

import jax
import jax.numpy as jnp
from jax import lax
from jax.experimental import pallas as pl
from jax.experimental.pallas import tpu as pltpu
from jax.sharding import PartitionSpec as P

time_step = 0.2
viscosity = 0.2
LANES = 128
CHUNK = 512
CENTRE = 1.1
LARGEST = 3.0 * 0.901
LEVELS = 32400.0
RELAY = (2.6, 0.65)
PARTIAL = (3.6, 0.65)
TOTAL = (6.5, 0.65)
SWEEP = (10.3, 0.8)


def kernel(pops, tiles, weights, terminal_in, history_in, initial_in, values, density_out,
           terminal, history, initial, load_sem, near, own_sum, part_out, part_in, cost_out, cost_in,
           value_out, start_value, mass_out, start_mass, swept, mass_main, slope_r, slope_c, sums_own, sums_all,
           near_send, near_recv, part_send, part_recv, cost_send, cost_recv, start_send, start_recv,
           back_send, back_recv, back_self):
    steps, rows, cols = history.shape
    width = cols // tiles
    full = width + LANES
    total_rows = tiles * rows
    outer = pops // 4
    me = lax.axis_index("tile")
    own = lax.axis_index("pop")
    core = own % 2
    plane = (own // 2) % 2
    line = own // 4

    def pop_of(a, b, c):
        return (a * 2 + b) * 2 + c

    partner = pop_of(line, plane, 1 - core)
    across = pop_of(line, 1 - plane, core)
    beyond = pop_of(line, 1 - plane, 1 - core)
    columns = [pop_of((line + j) % outer, plane, core) for j in range(1, outer)]
    peers = [(me + d) % tiles for d in range(1, tiles)]

    barrier = pltpu.get_barrier_semaphore()
    greeted = [{"tile": z} for z in peers] + [{"pop": q} for q in [partner, across] + columns]
    for there in greeted:
        pl.semaphore_signal(barrier, inc=1, device_id=there, device_id_type=pl.DeviceIdType.MESH)

    loads = [pltpu.make_async_copy(src, dst, load_sem.at[n]) for n, (src, dst) in enumerate(
        [(terminal_in, terminal), (initial_in, initial), (history_in, history)])]
    for load in loads:
        load.start()
    for load in loads:
        load.wait()
    right_side = lax.broadcasted_iota(jnp.int32, (rows, LANES), 1) < LANES // 2

    def main_of(block, z):
        return block[:, z * width:(z + 1) * width]

    def rim_of(block, z):
        right = ((z + 1) % tiles) * width
        left = ((z + tiles - 1) % tiles) * width + width - LANES
        return jnp.where(right_side, block[:, right:right + LANES], block[:, left:left + LANES])

    for src, dst in [(terminal, value_out), (initial, mass_out)]:
        block = src[...]
        for z in range(tiles):
            dst[z, :, :width] = main_of(block, z)
            dst[z, :, width:] = rim_of(block, z)
    start_value[me] = value_out[me]
    start_mass[me] = mass_out[me]

    pl.semaphore_wait(barrier, len(greeted))

    def cut(z):
        return pl.ds(pl.multiple_of(z * width, LANES), width)

    sent = []

    def remote(src, dst, send, recv, there):
        copy = pltpu.make_async_remote_copy(src_ref=src, dst_ref=dst, send_sem=send, recv_sem=recv,
                                            device_id=there, device_id_type=pl.DeviceIdType.MESH)
        copy.start()
        return copy

    def arrived(ref, sem):
        pltpu.make_async_copy(ref, ref, sem).wait()

    def spread(src, dst, send, recv):
        for z in peers:
            remote(src.at[z], dst.at[me], send, recv, {"tile": z})

    def wait_spread(dst, sem):
        arrived(dst.at[pl.ds(0, tiles - 1)], sem)

    for n in range(steps):
        t = steps - 1 - n
        sent.append(remote(history.at[t], near.at[1, t], near_send.at[1, n], near_recv.at[1, n], {"pop": across}))
        sent.append(remote(history.at[t], near.at[0, t], near_send.at[0, n], near_recv.at[0, n], {"pop": partner}))
    spread(value_out, start_value, start_send.at[0], start_recv.at[0])
    spread(mass_out, start_mass, start_send.at[1], start_recv.at[1])

    def weight(p, q):
        return weights[p, q].astype(jnp.float32) * (1.0 / pops)

    sources = [own, partner, across, beyond]
    own_weights = [weight(own, q) for q in sources]
    line_weights = [[weight(p, q) for q in sources] for p in columns]
    part_step = LARGEST * 4.0 / pops / LEVELS
    cost_step = LARGEST / LEVELS

    def coded(x, step):
        return jnp.round(x * (1.0 / step)).astype(jnp.int32).astype(jnp.int16)

    def decoded(x, step):
        return x.astype(jnp.int32).astype(jnp.float32) * step

    def stage_relay(n):
        t = steps - 1 - n
        arrived(near.at[1, t], near_recv.at[1, n])
        sent.append(remote(near.at[1, t], near.at[2, t], near_send.at[2, n], near_recv.at[2, n], {"pop": partner}))

    def stage_partial(n):
        t = steps - 1 - n
        arrived(near.at[0, t], near_recv.at[0, n])
        arrived(near.at[2, t], near_recv.at[2, n])
        for c in range(0, cols, CHUNK):
            span = slice(c, c + CHUNK)
            blocks = [history[t, :, span], near[0, t, :, span], near[1, t, :, span], near[2, t, :, span]]
            blocks = [b.astype(jnp.float32) - CENTRE for b in blocks]

            def mixed(factors):
                total = factors[0] * blocks[0]
                for f, b in zip(factors[1:], blocks[1:]):
                    total = total + f * b
                return total

            for j in range(outer - 1):
                part_out[j, n, :, span] = coded(mixed(line_weights[j]), part_step)
            own_sum[n, :, span] = mixed(own_weights)
        for j, q in enumerate(columns):
            sent.append(remote(part_out.at[j, n], part_in.at[j, n], part_send.at[j, n], part_recv.at[j, n], {"pop": q}))

    def stage_total(n):
        total = own_sum[n]
        for j in range(outer - 1):
            arrived(part_in.at[j, n], part_recv.at[j, n])
            total = total + decoded(part_in[j, n], part_step)
        for z in range(tiles):
            cost_out[n, z, :, :width] = coded(main_of(total, z), cost_step)
            cost_out[n, z, :, width:] = coded(rim_of(total, z), cost_step)
        spread(cost_out.at[n], cost_in.at[n], cost_send.at[n], cost_recv.at[n])
        cost_in[n, me] = cost_out[n, me]

    def ahead_r(x):
        return pltpu.roll(x, total_rows - 1, 0)

    def behind_r(x):
        return pltpu.roll(x, 1, 0)

    def ahead_c(x):
        return pltpu.roll(x, full - 1, 1)

    def behind_c(x):
        return pltpu.roll(x, 1, 1)

    def send_back(src, dst, n):
        pltpu.make_async_copy(src.at[me], dst.at[:, cut(me)], back_self.at[n]).start()
        for z in peers:
            remote(src.at[z], dst.at[:, cut(me)], back_send.at[n], back_recv.at[n], {"tile": z})

    def wait_back(src, dst, n):
        pltpu.make_async_copy(src.at[me], dst.at[:, cut(me)], back_self.at[n]).wait()
        landed = dst.at[:, pl.ds(0, (tiles - 1) * width)]
        arrived(landed, back_recv.at[n])
        arrived(landed, back_send.at[n])

    state = {}

    def stage_sweep(n):
        t = steps - 1 - n
        if n == 0:
            wait_spread(start_value, start_recv.at[0])
            state["u"] = start_value[...].reshape(total_rows, full)
        wait_spread(cost_in.at[n], cost_recv.at[n])
        source = decoded(cost_in[n], cost_step).reshape(total_rows, full)
        u = state["u"]
        dr = ahead_r(u) - u
        dc = ahead_c(u) - u
        if t + 1 < steps:
            slope_r[t + 1] = dr
            slope_c[t + 1] = dc
        er, ec = behind_r(dr), behind_c(dc)
        br, bc = jnp.maximum(er, 0.0), jnp.maximum(ec, 0.0)
        ar, ac = jnp.minimum(dr, 0.0), jnp.minimum(dc, 0.0)
        lap = (dr - er) + (dc - ec)
        ham = 0.5 * ((br * br + ar * ar) + (bc * bc + ac * ac))
        u = u + time_step * (viscosity * lap - ham + source)
        state["u"] = u
        main = u[:, :width]
        swept[t] = main.reshape(tiles, rows, width)
        send_back(swept.at[t], values.at[t], t)
        line_sum = jnp.sum(main, axis=0, keepdims=True)
        folded = line_sum[:, :LANES]
        for j in range(1, width // LANES):
            folded = folded + line_sum[:, j * LANES:(j + 1) * LANES]
        sums_own[t:t + 1, :] = folded

    stages = [(RELAY, stage_relay), (PARTIAL, stage_partial), (TOTAL, stage_total), (SWEEP, stage_sweep)]
    plan = sorted((first + per * n, k, n) for k, ((first, per), _) in enumerate(stages) for n in range(steps))
    for _, k, n in plan:
        stages[k][1](n)

    sums_n = steps + 1
    sums_all[me] = sums_own[...]
    for z in peers:
        remote(sums_own, sums_all.at[me], back_send.at[sums_n], back_recv.at[sums_n], {"tile": z})

    wait_spread(start_mass, start_recv.at[1])
    u = state["u"]
    mass = start_mass[...].reshape(total_rows, full)
    for t in range(steps):
        if t == 0:
            dr, dc = ahead_r(u) - u, ahead_c(u) - u
        else:
            dr, dc = slope_r[t], slope_c[t]
        mr, mc = ahead_r(mass), ahead_c(mass)
        flux_r = jnp.maximum(-dr, 0.0) * mass + jnp.minimum(-dr, 0.0) * mr
        flux_c = jnp.maximum(-dc, 0.0) * mass + jnp.minimum(-dc, 0.0) * mc
        net_r = viscosity * (mr - mass) - flux_r
        net_c = viscosity * (mc - mass) - flux_c
        mass = mass + time_step * ((net_r - behind_r(net_r)) + (net_c - behind_c(net_c)))
    mass_main[...] = mass[:, :width].reshape(tiles, rows, width)
    send_back(mass_main, density_out, steps)

    arrived(sums_all.at[pl.ds(0, tiles - 1)], back_recv.at[sums_n])
    arrived(sums_all.at[pl.ds(0, tiles - 1)], back_send.at[sums_n])
    grand = jnp.sum(jnp.sum(sums_all[...], axis=0), axis=1, keepdims=True) * (1.0 / (total_rows * cols))
    for t in reversed(range(steps)):
        wait_back(swept.at[t], values.at[t], t)
        values[t] = values[t] - grand[t:t + 1, :]
    wait_back(mass_main, density_out, steps)
    wait_spread(start_value, start_send.at[0])
    wait_spread(start_mass, start_send.at[1])
    for n in range(steps):
        wait_spread(cost_in.at[n], cost_send.at[n])
    for copy in sent:
        copy.wait_send()


def finish(values, density, values_out, density_out, sems):
    copies = [
        pltpu.make_async_copy(values, values_out, sems.at[0]),
        pltpu.make_async_copy(density, density_out, sems.at[1]),
    ]
    for copy in copies:
        copy.start()
    for copy in copies:
        copy.wait()


def per_device(pops, tiles, weights, terminal, density_history, density_init):
    _, steps, rows, cols = density_history.shape
    width = cols // tiles
    outer = pops // 4
    total_rows = tiles * rows
    full = width + LANES
    dma = pltpu.SemaphoreType.DMA
    lines = max(outer - 1, 1)
    vmem = pl.BlockSpec(memory_space=pltpu.VMEM)
    anywhere = pl.BlockSpec(memory_space=pl.ANY)
    values, density = pl.pallas_call(
        functools.partial(kernel, pops, tiles),
        out_shape=(
            pltpu.VMEM((steps, rows, cols), jnp.float32),
            pltpu.VMEM((rows, cols), jnp.float32),
        ),
        in_specs=[pl.BlockSpec(memory_space=pltpu.SMEM), anywhere, anywhere, anywhere],
        out_specs=(vmem, vmem),
        scratch_shapes=[
            pltpu.VMEM((rows, cols), jnp.float32),
            pltpu.VMEM((steps, rows, cols), jnp.bfloat16),
            pltpu.VMEM((rows, cols), jnp.float32),
            dma((3,)),
            pltpu.VMEM((3, steps, rows, cols), jnp.bfloat16),
            pltpu.VMEM((steps, rows, cols), jnp.float32),
            pltpu.VMEM((lines, steps, rows, cols), jnp.int16),
            pltpu.VMEM((lines, steps, rows, cols), jnp.int16),
            pltpu.VMEM((steps, tiles, rows, full), jnp.int16),
            pltpu.VMEM((steps, tiles, rows, full), jnp.int16),
            pltpu.VMEM((tiles, rows, full), jnp.float32),
            pltpu.VMEM((tiles, rows, full), jnp.float32),
            pltpu.VMEM((tiles, rows, full), jnp.float32),
            pltpu.VMEM((tiles, rows, full), jnp.float32),
            pltpu.VMEM((steps, tiles, rows, width), jnp.float32),
            pltpu.VMEM((tiles, rows, width), jnp.float32),
            pltpu.VMEM((steps, total_rows, full), jnp.float32),
            pltpu.VMEM((steps, total_rows, full), jnp.float32),
            pltpu.VMEM((steps, LANES), jnp.float32),
            pltpu.VMEM((tiles, steps, LANES), jnp.float32),
            dma((3, steps)), dma((3, steps)),
            dma((lines, steps)), dma((lines, steps)),
            dma((steps,)), dma((steps,)),
            dma((2,)), dma((2,)),
            dma((steps + 2,)), dma((steps + 2,)), dma((steps + 1,)),
        ],
        compiler_params=pltpu.CompilerParams(collective_id=0, has_side_effects=True),
    )(weights, terminal[0], density_history[0], density_init[0])
    values, density = pl.pallas_call(
        finish,
        out_shape=(
            jax.ShapeDtypeStruct((steps, rows, cols), jnp.float32),
            jax.ShapeDtypeStruct((rows, cols), jnp.float32),
        ),
        in_specs=[anywhere, anywhere],
        out_specs=(anywhere, anywhere),
        scratch_shapes=[dma((2,))],
        compiler_params=pltpu.CompilerParams(vmem_limit_bytes=8 * 1024 * 1024),
    )(values, density)
    return values[None], density[None]


def solution(mesh):
    in_specs = (P(), P("pop", "tile", None), P("pop", None, "tile", None), P("pop", "tile", None))
    out_specs = (P("pop", None, "tile", None), P("pop", "tile", None))
    body = functools.partial(per_device, mesh.shape["pop"], mesh.shape["tile"])
    return jax.shard_map(body, mesh=mesh, in_specs=in_specs, out_specs=out_specs, check_vma=False)
```

time: 36.8 us -> 38.3 us (1.041)
  Pallas kernels: 35.9 us -> 37.5 us
    pallas_call x1, Pallas kernels: 35.1 us -> 36.7 us  [per_device(): pl.pallas_call(functools.partial(kernel, pops, tiles), out_shape=(pltpu.V...]
where the time goes in v1:
time: 38.3 us; the launch traced here: 38.2 us
  Pallas kernels  37.5 us (98%)
  between operations  0.64 us (2%)
    pallas_call x1, Pallas kernels, per_device(): pl.pallas_call(functools.partial(kernel, pops, tiles), out_shape=(pltpu.V...  36.7 us
    pallas_call x1, Pallas kernels, per_device(): pl.pallas_call(finish, out_shape=(jax.ShapeDtypeStruct((steps, rows, cols...  0.82 us

profile of v1, /device:TPU:0, one launch (start us, length us, event | category | flops | bytes accessed | tf_op | source)
XLA Modules:
  0.0 38.2 jit_solution(11739292764209703515)
XLA Ops:
  0.6 36.7 %shard_map.59 = (f32[8,8,2048]{2,1,0:T(8,128)S(1)}, f32[8,2048]{1,0:T(8,128)S(1)}) custom-call(s32[8,8]{1,0:T(8,128)} %weights.1, f32[8,2048]{1,0:T(8,128)} %bitcast.6, bf16[8,8,2048]{2,1,0:T(8,128)(2,1)} %bitcast.5, f32[8,2048]{1,0:T(8,128)} %bitcast.7), custom_call_target="tpu_custom_call" | custom-call | tf_op jit(solution)/shard_map/pallas_call | solution.py:276
  37.3 0.8 %shard_map.60 = (f32[8,8,2048]{2,1,0:T(8,128)}, f32[8,2048]{1,0:T(8,128)}) custom-call(f32[8,8,2048]{2,1,0:T(8,128)S(1)} %get-tuple-element.6.values, f32[8,2048]{1,0:T(8,128)S(1)} %get-tuple-element.7.density), custom_call_target="tpu_custom_call" | custom-call | tf_op jit(solution)/shard_map/pallas_call | solution.py:313

commit v2 on v1

--- a/solution.py
+++ b/solution.py
@@ -17,14 +17,15 @@
 RELAY = (2.6, 0.65)
 PARTIAL = (3.6, 0.65)
 TOTAL = (6.5, 0.65)
-SWEEP = (10.3, 0.8)
-
-
-def kernel(pops, tiles, weights, terminal_in, history_in, initial_in, values, density_out,
-           terminal, history, initial, load_sem, near, own_sum, part_out, part_in, cost_out, cost_in,
-           value_out, start_value, mass_out, start_mass, swept, mass_main, slope_r, slope_c, sums_own, sums_all,
+SWEEP = (10.3, 0.65)
+STRIP = (14.0, 0.65)
+
+
+def kernel(pops, tiles, weights_in, terminal_in, history_in, initial_in, values, density_out,
+           weights, terminal, history, initial, load_sem, near, own_sum, part_out, part_in, cost_out, cost_in,
+           value_out, start_value, mass_out, start_mass, edge_out, edge_in, mass_main, slope_r, slope_c, sums_own, sums_all,
            near_send, near_recv, part_send, part_recv, cost_send, cost_recv, start_send, start_recv,
-           back_send, back_recv, back_self):
+           edge_send, edge_recv, back_send, back_recv, back_self):
     steps, rows, cols = history.shape
     width = cols // tiles
     full = width + LANES
@@ -51,7 +52,7 @@
         pl.semaphore_signal(barrier, inc=1, device_id=there, device_id_type=pl.DeviceIdType.MESH)
 
     loads = [pltpu.make_async_copy(src, dst, load_sem.at[n]) for n, (src, dst) in enumerate(
-        [(terminal_in, terminal), (initial_in, initial), (history_in, history)])]
+        [(weights_in, weights), (terminal_in, terminal), (initial_in, initial), (history_in, history)])]
     for load in loads:
         load.start()
     for load in loads:
@@ -150,6 +151,7 @@
         for j in range(outer - 1):
             arrived(part_in.at[j, n], part_recv.at[j, n])
             total = total + decoded(part_in[j, n], part_step)
+        own_sum[n] = total
         for z in range(tiles):
             cost_out[n, z, :, :width] = coded(main_of(total, z), cost_step)
             cost_out[n, z, :, width:] = coded(rim_of(total, z), cost_step)
@@ -168,6 +170,15 @@
     def behind_c(x):
         return pltpu.roll(x, 1, 1)
 
+    def send_edges(main, n):
+        for z in range(tiles):
+            above = (z * rows + total_rows - 1) % total_rows
+            below = (z * rows + rows) % total_rows
+            edge_out[n, z, 0:1, :] = main[above:above + 1, :]
+            edge_out[n, z, 1:2, :] = main[below:below + 1, :]
+        spread(edge_out.at[n], edge_in.at[n], edge_send.at[n], edge_recv.at[n])
+        edge_in[n, me] = edge_out[n, me]
+
     def send_back(src, dst, n):
         pltpu.make_async_copy(src.at[me], dst.at[:, cut(me)], back_self.at[n]).start()
         for z in peers:
@@ -186,6 +197,7 @@
         if n == 0:
             wait_spread(start_value, start_recv.at[0])
             state["u"] = start_value[...].reshape(total_rows, full)
+            send_edges(state["u"][:, :width], 0)
         wait_spread(cost_in.at[n], cost_recv.at[n])
         source = decoded(cost_in[n], cost_step).reshape(total_rows, full)
         u = state["u"]
@@ -202,20 +214,39 @@
         u = u + time_step * (viscosity * lap - ham + source)
         state["u"] = u
         main = u[:, :width]
-        swept[t] = main.reshape(tiles, rows, width)
-        send_back(swept.at[t], values.at[t], t)
+        if t > 0:
+            send_edges(main, n + 1)
         line_sum = jnp.sum(main, axis=0, keepdims=True)
         folded = line_sum[:, :LANES]
         for j in range(1, width // LANES):
             folded = folded + line_sum[:, j * LANES:(j + 1) * LANES]
         sums_own[t:t + 1, :] = folded
 
-    stages = [(RELAY, stage_relay), (PARTIAL, stage_partial), (TOTAL, stage_total), (SWEEP, stage_sweep)]
+    row = lax.broadcasted_iota(jnp.int32, (rows, cols), 0)
+
+    def stage_strip(n):
+        t = steps - 1 - n
+        wait_spread(edge_in.at[n], edge_recv.at[n])
+        above = jnp.concatenate([edge_in[n, z, 0:1, :] for z in range(tiles)], axis=1)
+        below = jnp.concatenate([edge_in[n, z, 1:2, :] for z in range(tiles)], axis=1)
+        u = terminal[...] if n == 0 else values[t + 1]
+        dr = jnp.where(row == rows - 1, below, pltpu.roll(u, rows - 1, 0)) - u
+        er = u - jnp.where(row == 0, above, pltpu.roll(u, 1, 0))
+        dc = pltpu.roll(u, cols - 1, 1) - u
+        ec = pltpu.roll(dc, 1, 1)
+        br, bc = jnp.maximum(er, 0.0), jnp.maximum(ec, 0.0)
+        ar, ac = jnp.minimum(dr, 0.0), jnp.minimum(dc, 0.0)
+        lap = (dr - er) + (dc - ec)
+        ham = 0.5 * ((br * br + ar * ar) + (bc * bc + ac * ac))
+        values[t] = u + time_step * (viscosity * lap - ham + own_sum[n])
+
+    stages = [(RELAY, stage_relay), (PARTIAL, stage_partial), (TOTAL, stage_total), (SWEEP, stage_sweep), (STRIP, stage_strip)]
     plan = sorted((first + per * n, k, n) for k, ((first, per), _) in enumerate(stages) for n in range(steps))
-    for _, k, n in plan:
+    last = plan.index((SWEEP[0] + SWEEP[1] * (steps - 1), 3, steps - 1)) + 1
+    for _, k, n in plan[:last]:
         stages[k][1](n)
 
-    sums_n = steps + 1
+    sums_n = 1
     sums_all[me] = sums_own[...]
     for z in peers:
         remote(sums_own, sums_all.at[me], back_send.at[sums_n], back_recv.at[sums_n], {"tile": z})
@@ -235,19 +266,21 @@
         net_c = viscosity * (mc - mass) - flux_c
         mass = mass + time_step * ((net_r - behind_r(net_r)) + (net_c - behind_c(net_c)))
     mass_main[...] = mass[:, :width].reshape(tiles, rows, width)
-    send_back(mass_main, density_out, steps)
+    send_back(mass_main, density_out, 0)
+    for _, k, n in plan[last:]:
+        stages[k][1](n)
 
     arrived(sums_all.at[pl.ds(0, tiles - 1)], back_recv.at[sums_n])
     arrived(sums_all.at[pl.ds(0, tiles - 1)], back_send.at[sums_n])
     grand = jnp.sum(jnp.sum(sums_all[...], axis=0), axis=1, keepdims=True) * (1.0 / (total_rows * cols))
     for t in reversed(range(steps)):
-        wait_back(swept.at[t], values.at[t], t)
         values[t] = values[t] - grand[t:t + 1, :]
-    wait_back(mass_main, density_out, steps)
+    wait_back(mass_main, density_out, 0)
     wait_spread(start_value, start_send.at[0])
     wait_spread(start_mass, start_send.at[1])
     for n in range(steps):
         wait_spread(cost_in.at[n], cost_send.at[n])
+        wait_spread(edge_in.at[n], edge_send.at[n])
     for copy in sent:
         copy.wait_send()
 
@@ -279,13 +312,14 @@
             pltpu.VMEM((steps, rows, cols), jnp.float32),
             pltpu.VMEM((rows, cols), jnp.float32),
         ),
-        in_specs=[pl.BlockSpec(memory_space=pltpu.SMEM), anywhere, anywhere, anywhere],
+        in_specs=[anywhere, anywhere, anywhere, anywhere],
         out_specs=(vmem, vmem),
         scratch_shapes=[
+            pltpu.SMEM((pops, pops), jnp.int32),
             pltpu.VMEM((rows, cols), jnp.float32),
             pltpu.VMEM((steps, rows, cols), jnp.bfloat16),
             pltpu.VMEM((rows, cols), jnp.float32),
-            dma((3,)),
+            dma((4,)),
             pltpu.VMEM((3, steps, rows, cols), jnp.bfloat16),
             pltpu.VMEM((steps, rows, cols), jnp.float32),
             pltpu.VMEM((lines, steps, rows, cols), jnp.int16),
@@ -296,7 +330,8 @@
             pltpu.VMEM((tiles, rows, full), jnp.float32),
             pltpu.VMEM((tiles, rows, full), jnp.float32),
             pltpu.VMEM((tiles, rows, full), jnp.float32),
-            pltpu.VMEM((steps, tiles, rows, width), jnp.float32),
+            pltpu.VMEM((steps, tiles, 2, width), jnp.float32),
+            pltpu.VMEM((steps, tiles, 2, width), jnp.float32),
             pltpu.VMEM((tiles, rows, width), jnp.float32),
             pltpu.VMEM((steps, total_rows, full), jnp.float32),
             pltpu.VMEM((steps, total_rows, full), jnp.float32),
@@ -306,7 +341,8 @@
             dma((lines, steps)), dma((lines, steps)),
             dma((steps,)), dma((steps,)),
             dma((2,)), dma((2,)),
-            dma((steps + 2,)), dma((steps + 2,)), dma((steps + 1,)),
+            dma((steps,)), dma((steps,)),
+            dma((2,)), dma((2,)), dma((1,)),
         ],
         compiler_params=pltpu.CompilerParams(collective_id=0, has_side_effects=True),
     )(weights, terminal[0], density_history[0], density_init[0])

time: 38.3 us -> 32.4 us (0.85)
  Pallas kernels: 37.5 us -> 31.6 us
    pallas_call x1, Pallas kernels: 36.7 us -> 30.8 us  [per_device(): pl.pallas_call(functools.partial(kernel, pops, tiles), out_shape=(pltpu.V...]
where the time goes in v2:
time: 32.4 us; the launch traced here: 32.2 us
  Pallas kernels  31.6 us (98%)
  between operations  0.64 us (2%)
    pallas_call x1, Pallas kernels, per_device(): pl.pallas_call(functools.partial(kernel, pops, tiles), out_shape=(pltpu.V...  30.8 us
    pallas_call x1, Pallas kernels, per_device(): pl.pallas_call(finish, out_shape=(jax.ShapeDtypeStruct((steps, rows, cols...  0.82 us

profile of v2, /device:TPU:0, one launch (start us, length us, event | category | flops | bytes accessed | tf_op | source)
XLA Modules:
  0.0 32.2 jit_solution(1322560632460173810)
XLA Ops:
  0.6 30.8 %shard_map.59 = (f32[8,8,2048]{2,1,0:T(8,128)S(1)}, f32[8,2048]{1,0:T(8,128)S(1)}) custom-call(s32[8,8]{1,0:T(8,128)} %weights_in.1, f32[8,2048]{1,0:T(8,128)} %bitcast.6, bf16[8,8,2048]{2,1,0:T(8,128)(2,1)} %bitcast.5, f32[8,2048]{1,0:T(8,128)} %bitcast.7), custom_call_target="tpu_custom_call" | custom-call | tf_op jit(solution)/shard_map/pallas_call | solution.py:309
  31.4 0.8 %shard_map.60 = (f32[8,8,2048]{2,1,0:T(8,128)}, f32[8,2048]{1,0:T(8,128)}) custom-call(f32[8,8,2048]{2,1,0:T(8,128)S(1)} %get-tuple-element.6.values, f32[8,2048]{1,0:T(8,128)S(1)} %get-tuple-element.7.density), custom_call_target="tpu_custom_call" | custom-call | tf_op jit(solution)/shard_map/pallas_call | solution.py:349

commit v3 on v2

--- a/solution.py
+++ b/solution.py
@@ -10,21 +10,24 @@
 time_step = 0.2
 viscosity = 0.2
 LANES = 128
+WINDOWS = 4
+SPAN = LANES // WINDOWS
 CHUNK = 512
 CENTRE = 1.1
 LARGEST = 3.0 * 0.901
 LEVELS = 32400.0
-RELAY = (2.6, 0.65)
-PARTIAL = (3.6, 0.65)
-TOTAL = (6.5, 0.65)
-SWEEP = (10.3, 0.65)
-STRIP = (14.0, 0.65)
+RELAY = (2.6, 0.35)
+PARTIAL = (3.6, 0.35)
+TOTAL = (6.4, 0.6)
+SWEEP = (12.5, 0.9)
+STRIP = (20.0, 0.65)
 
 
 def kernel(pops, tiles, weights_in, terminal_in, history_in, initial_in, values, density_out,
-           weights, terminal, history, initial, load_sem, near, own_sum, part_out, part_in, cost_out, cost_in,
-           value_out, start_value, mass_out, start_mass, edge_out, edge_in, mass_main, slope_r, slope_c, sums_own, sums_all,
-           near_send, near_recv, part_send, part_recv, cost_send, cost_recv, start_send, start_recv,
+           weights, terminal, history, initial, load_sem, near_other, near, near_relay, own_sum, part_out, part_in,
+           cost_out, cost_in, rim_out, rim_in, value_out, start_value, mass_out, start_mass, edge_out, edge_in, mass_main, slope_r, slope_c, sums_own, sums_all,
+           other_send, other_recv, near_send, near_recv, relay_send, relay_recv, part_send, part_recv,
+           cost_send, cost_recv, rim_send, rim_recv, start_send, start_recv,
            edge_send, edge_recv, back_send, back_recv, back_self):
     steps, rows, cols = history.shape
     width = cols // tiles
@@ -42,8 +45,22 @@
 
     partner = pop_of(line, plane, 1 - core)
     across = pop_of(line, 1 - plane, core)
-    beyond = pop_of(line, 1 - plane, 1 - core)
     columns = [pop_of((line + j) % outer, plane, core) for j in range(1, outer)]
+    behind = [(line + outer - j) % outer for j in range(1, outer)]
+
+    def along_row(n):
+        return n % 2 == 0 or outer == 1
+
+    def first_peers(n):
+        return [across] if along_row(n) else columns
+
+    def second_peers(n):
+        return columns if along_row(n) else [across]
+
+    def sources(n):
+        far = [(line, 1 - plane)] if along_row(n) else [(a, plane) for a in behind]
+        return [own, partner] + [pop_of(a, b, core) for a, b in far] + [pop_of(a, b, 1 - core) for a, b in far]
+
     peers = [(me + d) % tiles for d in range(1, tiles)]
 
     barrier = pltpu.get_barrier_semaphore()
@@ -57,6 +74,8 @@
         load.start()
     for load in loads:
         load.wait()
+    lane = lax.broadcasted_iota(jnp.int32, (rows, LANES), 1)
+    window = ((lane + SPAN // 2) % LANES) // SPAN
     right_side = lax.broadcasted_iota(jnp.int32, (rows, LANES), 1) < LANES // 2
 
     def main_of(block, z):
@@ -100,18 +119,18 @@
 
     for n in range(steps):
         t = steps - 1 - n
-        sent.append(remote(history.at[t], near.at[1, t], near_send.at[1, n], near_recv.at[1, n], {"pop": across}))
-        sent.append(remote(history.at[t], near.at[0, t], near_send.at[0, n], near_recv.at[0, n], {"pop": partner}))
+        for j, q in enumerate(first_peers(n)):
+            sent.append(remote(history.at[t], near.at[j, t], near_send.at[j, n], near_recv.at[j, n], {"pop": q}))
+        sent.append(remote(history.at[t], near_other.at[t], other_send.at[n], other_recv.at[n], {"pop": partner}))
     spread(value_out, start_value, start_send.at[0], start_recv.at[0])
     spread(mass_out, start_mass, start_send.at[1], start_recv.at[1])
 
     def weight(p, q):
         return weights[p, q].astype(jnp.float32) * (1.0 / pops)
 
-    sources = [own, partner, across, beyond]
-    own_weights = [weight(own, q) for q in sources]
-    line_weights = [[weight(p, q) for q in sources] for p in columns]
-    part_step = LARGEST * 4.0 / pops / LEVELS
+    def part_step(n):
+        return LARGEST * (4.0 if along_row(n) else 2.0 * outer) / pops / LEVELS
+
     cost_step = LARGEST / LEVELS
 
     def coded(x, step):
@@ -122,16 +141,23 @@
 
     def stage_relay(n):
         t = steps - 1 - n
-        arrived(near.at[1, t], near_recv.at[1, n])
-        sent.append(remote(near.at[1, t], near.at[2, t], near_send.at[2, n], near_recv.at[2, n], {"pop": partner}))
+        for j in range(len(first_peers(n))):
+            arrived(near.at[j, t], near_recv.at[j, n])
+            sent.append(remote(near.at[j, t], near_relay.at[j, t], relay_send.at[j, n], relay_recv.at[j, n],
+                               {"pop": partner}))
 
     def stage_partial(n):
         t = steps - 1 - n
-        arrived(near.at[0, t], near_recv.at[0, n])
-        arrived(near.at[2, t], near_recv.at[2, n])
+        far = range(len(first_peers(n)))
+        arrived(near_other.at[t], other_recv.at[n])
+        for j in far:
+            arrived(near_relay.at[j, t], relay_recv.at[j, n])
+        own_factors = [weight(own, q) for q in sources(n)]
+        part_factors = [[weight(p, q) for q in sources(n)] for p in second_peers(n)]
         for c in range(0, cols, CHUNK):
             span = slice(c, c + CHUNK)
-            blocks = [history[t, :, span], near[0, t, :, span], near[1, t, :, span], near[2, t, :, span]]
+            blocks = [history[t, :, span], near_other[t, :, span]]
+            blocks += [near[j, t, :, span] for j in far] + [near_relay[j, t, :, span] for j in far]
             blocks = [b.astype(jnp.float32) - CENTRE for b in blocks]
 
             def mixed(factors):
@@ -140,23 +166,31 @@
                     total = total + f * b
                 return total
 
-            for j in range(outer - 1):
-                part_out[j, n, :, span] = coded(mixed(line_weights[j]), part_step)
-            own_sum[n, :, span] = mixed(own_weights)
-        for j, q in enumerate(columns):
+            for j, factors in enumerate(part_factors):
+                part_out[j, n, :, span] = coded(mixed(factors), part_step(n))
+            own_sum[n, :, span] = mixed(own_factors)
+        for j, q in enumerate(second_peers(n)):
             sent.append(remote(part_out.at[j, n], part_in.at[j, n], part_send.at[j, n], part_recv.at[j, n], {"pop": q}))
 
     def stage_total(n):
         total = own_sum[n]
-        for j in range(outer - 1):
+        for j in range(len(second_peers(n))):
             arrived(part_in.at[j, n], part_recv.at[j, n])
-            total = total + decoded(part_in[j, n], part_step)
+            total = total + decoded(part_in[j, n], part_step(n))
         own_sum[n] = total
         for z in range(tiles):
-            cost_out[n, z, :, :width] = coded(main_of(total, z), cost_step)
-            cost_out[n, z, :, width:] = coded(rim_of(total, z), cost_step)
+            cost_out[n, z] = coded(main_of(total, z), cost_step)
         spread(cost_out.at[n], cost_in.at[n], cost_send.at[n], cost_recv.at[n])
         cost_in[n, me] = cost_out[n, me]
+        g, k = n // WINDOWS, n % WINDOWS
+        if k == WINDOWS - 1:
+            for z in range(tiles):
+                rim = rim_of(own_sum[g * WINDOWS], z)
+                for i in range(1, WINDOWS):
+                    rim = jnp.where(window == i, pltpu.roll(rim_of(own_sum[g * WINDOWS + i], z), SPAN * i, 1), rim)
+                rim_out[g, z] = coded(rim, cost_step)
+            spread(rim_out.at[g], rim_in.at[g], rim_send.at[g], rim_recv.at[g])
+            rim_in[g, me] = rim_out[g, me]
 
     def ahead_r(x):
         return pltpu.roll(x, total_rows - 1, 0)
@@ -199,7 +233,12 @@
             state["u"] = start_value[...].reshape(total_rows, full)
             send_edges(state["u"][:, :width], 0)
         wait_spread(cost_in.at[n], cost_recv.at[n])
-        source = decoded(cost_in[n], cost_step).reshape(total_rows, full)
+        g, k = n // WINDOWS, n % WINDOWS
+        if k == 0:
+            wait_spread(rim_in.at[g], rim_recv.at[g])
+            state["rim"] = decoded(rim_in[g], cost_step).reshape(total_rows, LANES)
+        rim = state["rim"] if k == 0 else pltpu.roll(state["rim"], LANES - SPAN * k, 1)
+        source = jnp.concatenate([decoded(cost_in[n], cost_step).reshape(total_rows, width), rim], axis=1)
         u = state["u"]
         dr = ahead_r(u) - u
         dc = ahead_c(u) - u
@@ -278,6 +317,8 @@
     wait_back(mass_main, density_out, 0)
     wait_spread(start_value, start_send.at[0])
     wait_spread(start_mass, start_send.at[1])
+    for g in range(steps // WINDOWS):
+        wait_spread(rim_in.at[g], rim_send.at[g])
     for n in range(steps):
         wait_spread(cost_in.at[n], cost_send.at[n])
         wait_spread(edge_in.at[n], edge_send.at[n])
@@ -304,6 +345,7 @@
     full = width + LANES
     dma = pltpu.SemaphoreType.DMA
     lines = max(outer - 1, 1)
+    groups = steps // WINDOWS
     vmem = pl.BlockSpec(memory_space=pltpu.VMEM)
     anywhere = pl.BlockSpec(memory_space=pl.ANY)
     values, density = pl.pallas_call(
@@ -320,12 +362,16 @@
             pltpu.VMEM((steps, rows, cols), jnp.bfloat16),
             pltpu.VMEM((rows, cols), jnp.float32),
             dma((4,)),
-            pltpu.VMEM((3, steps, rows, cols), jnp.bfloat16),
+            pltpu.VMEM((steps, rows, cols), jnp.bfloat16),
+            pltpu.VMEM((lines, steps, rows, cols), jnp.bfloat16),
+            pltpu.VMEM((lines, steps, rows, cols), jnp.bfloat16),
             pltpu.VMEM((steps, rows, cols), jnp.float32),
             pltpu.VMEM((lines, steps, rows, cols), jnp.int16),
             pltpu.VMEM((lines, steps, rows, cols), jnp.int16),
-            pltpu.VMEM((steps, tiles, rows, full), jnp.int16),
-            pltpu.VMEM((steps, tiles, rows, full), jnp.int16),
+            pltpu.VMEM((steps, tiles, rows, width), jnp.int16),
+            pltpu.VMEM((steps, tiles, rows, width), jnp.int16),
+            pltpu.VMEM((groups, tiles, rows, LANES), jnp.int16),
+            pltpu.VMEM((groups, tiles, rows, LANES), jnp.int16),
             pltpu.VMEM((tiles, rows, full), jnp.float32),
             pltpu.VMEM((tiles, rows, full), jnp.float32),
             pltpu.VMEM((tiles, rows, full), jnp.float32),
@@ -337,9 +383,12 @@
             pltpu.VMEM((steps, total_rows, full), jnp.float32),
             pltpu.VMEM((steps, LANES), jnp.float32),
             pltpu.VMEM((tiles, steps, LANES), jnp.float32),
-            dma((3, steps)), dma((3, steps)),
+            dma((steps,)), dma((steps,)),
+            dma((lines, steps)), dma((lines, steps)),
+            dma((lines, steps)), dma((lines, steps)),
             dma((lines, steps)), dma((lines, steps)),
             dma((steps,)), dma((steps,)),
+            dma((groups,)), dma((groups,)),
             dma((2,)), dma((2,)),
             dma((steps,)), dma((steps,)),
             dma((2,)), dma((2,)), dma((1,)),

time: 32.4 us -> 30.4 us (0.938)
  Pallas kernels: 31.6 us -> 29.6 us
    pallas_call x1, Pallas kernels: 30.8 us -> 28.8 us  [per_device(): pl.pallas_call(functools.partial(kernel, pops, tiles), out_shape=(pltpu.V...]
where the time goes in v3:
time: 30.4 us; the launch traced here: 30.3 us
  Pallas kernels  29.6 us (97%)
  between operations  0.64 us (2%)
    pallas_call x1, Pallas kernels, per_device(): pl.pallas_call(functools.partial(kernel, pops, tiles), out_shape=(pltpu.V...  28.8 us
    pallas_call x1, Pallas kernels, per_device(): pl.pallas_call(finish, out_shape=(jax.ShapeDtypeStruct((steps, rows, cols...  0.82 us

profile of v3, /device:TPU:0, one launch (start us, length us, event | category | flops | bytes accessed | tf_op | source)
XLA Modules:
  0.0 30.3 jit_solution(9284801720692006730)
XLA Ops:
  0.6 28.8 %shard_map.59 = (f32[8,8,2048]{2,1,0:T(8,128)S(1)}, f32[8,2048]{1,0:T(8,128)S(1)}) custom-call(s32[8,8]{1,0:T(8,128)} %weights_in.1, f32[8,2048]{1,0:T(8,128)} %bitcast.6, bf16[8,8,2048]{2,1,0:T(8,128)(2,1)} %bitcast.5, f32[8,2048]{1,0:T(8,128)} %bitcast.7), custom_call_target="tpu_custom_call" | custom-call | tf_op jit(solution)/shard_map/pallas_call | solution.py:351
  29.4 0.8 %shard_map.60 = (f32[8,8,2048]{2,1,0:T(8,128)}, f32[8,2048]{1,0:T(8,128)}) custom-call(f32[8,8,2048]{2,1,0:T(8,128)S(1)} %get-tuple-element.6.values, f32[8,2048]{1,0:T(8,128)S(1)} %get-tuple-element.7.density), custom_call_target="tpu_custom_call" | custom-call | tf_op jit(solution)/shard_map/pallas_call | solution.py:398

commit v4 on v3

--- a/solution.py
+++ b/solution.py
@@ -173,6 +173,9 @@
             sent.append(remote(part_out.at[j, n], part_in.at[j, n], part_send.at[j, n], part_recv.at[j, n], {"pop": q}))
 
     def stage_total(n):
+        if n == 0:
+            wait_spread(start_value, start_recv.at[0])
+            send_edges(start_value[:, :, :width].reshape(total_rows, width), 0)
         total = own_sum[n]
         for j in range(len(second_peers(n))):
             arrived(part_in.at[j, n], part_recv.at[j, n])
@@ -229,9 +232,7 @@
     def stage_sweep(n):
         t = steps - 1 - n
         if n == 0:
-            wait_spread(start_value, start_recv.at[0])
             state["u"] = start_value[...].reshape(total_rows, full)
-            send_edges(state["u"][:, :width], 0)
         wait_spread(cost_in.at[n], cost_recv.at[n])
         g, k = n // WINDOWS, n % WINDOWS
         if k == 0:
@@ -298,12 +299,13 @@
             dr, dc = ahead_r(u) - u, ahead_c(u) - u
         else:
             dr, dc = slope_r[t], slope_c[t]
-        mr, mc = ahead_r(mass), ahead_c(mass)
-        flux_r = jnp.maximum(-dr, 0.0) * mass + jnp.minimum(-dr, 0.0) * mr
-        flux_c = jnp.maximum(-dc, 0.0) * mass + jnp.minimum(-dc, 0.0) * mc
-        net_r = viscosity * (mr - mass) - flux_r
-        net_c = viscosity * (mc - mass) - flux_c
-        mass = mass + time_step * ((net_r - behind_r(net_r)) + (net_c - behind_c(net_c)))
+        pr, qr = viscosity + jnp.maximum(dr, 0.0), viscosity + jnp.maximum(-dr, 0.0)
+        pc, qc = viscosity + jnp.maximum(dc, 0.0), viscosity + jnp.maximum(-dc, 0.0)
+        ec = behind_c(dc)
+        bc, kc = viscosity + jnp.maximum(ec, 0.0), viscosity + jnp.maximum(-ec, 0.0)
+        net_r = pr * ahead_r(mass) - qr * mass
+        net_c = (pc * ahead_c(mass) - qc * mass) - (bc * mass - kc * behind_c(mass))
+        mass = mass + time_step * ((net_r - behind_r(net_r)) + net_c)
     mass_main[...] = mass[:, :width].reshape(tiles, rows, width)
     send_back(mass_main, density_out, 0)
     for _, k, n in plan[last:]:

time: 30.4 us -> 29.9 us (0.984)
  Pallas kernels: 29.6 us -> 29.1 us
    pallas_call x1, Pallas kernels: 28.8 us -> 28.3 us  [per_device(): pl.pallas_call(functools.partial(kernel, pops, tiles), out_shape=(pltpu.V...]
where the time goes in v4:
time: 29.9 us; the launch traced here: 29.7 us
  Pallas kernels  29.1 us (97%)
  between operations  0.64 us (2%)
    pallas_call x1, Pallas kernels, per_device(): pl.pallas_call(functools.partial(kernel, pops, tiles), out_shape=(pltpu.V...  28.3 us
    pallas_call x1, Pallas kernels, per_device(): pl.pallas_call(finish, out_shape=(jax.ShapeDtypeStruct((steps, rows, cols...  0.82 us

profile of v4, /device:TPU:0, one launch (start us, length us, event | category | flops | bytes accessed | tf_op | source)
XLA Modules:
  0.0 29.7 jit_solution(7427495291885023574)
XLA Ops:
  0.6 28.3 %shard_map.59 = (f32[8,8,2048]{2,1,0:T(8,128)S(1)}, f32[8,2048]{1,0:T(8,128)S(1)}) custom-call(s32[8,8]{1,0:T(8,128)} %weights_in.1, f32[8,2048]{1,0:T(8,128)} %bitcast.6, bf16[8,8,2048]{2,1,0:T(8,128)(2,1)} %bitcast.5, f32[8,2048]{1,0:T(8,128)} %bitcast.7), custom_call_target="tpu_custom_call" | custom-call | tf_op jit(solution)/shard_map/pallas_call | solution.py:353
  28.9 0.8 %shard_map.60 = (f32[8,8,2048]{2,1,0:T(8,128)}, f32[8,2048]{1,0:T(8,128)}) custom-call(f32[8,8,2048]{2,1,0:T(8,128)S(1)} %get-tuple-element.6.values, f32[8,2048]{1,0:T(8,128)S(1)} %get-tuple-element.7.density), custom_call_target="tpu_custom_call" | custom-call | tf_op jit(solution)/shard_map/pallas_call | solution.py:400

commit v5 on v4

--- a/solution.py
+++ b/solution.py
@@ -13,6 +13,7 @@
 WINDOWS = 4
 SPAN = LANES // WINDOWS
 CHUNK = 512
+BOTH = (0, 1)
 CENTRE = 1.1
 LARGEST = 3.0 * 0.901
 LEVELS = 32400.0
@@ -54,6 +55,9 @@
     def first_peers(n):
         return [across] if along_row(n) else columns
 
+    def flipped(q):
+        return q + 1 - 2 * (q % 2)
+
     def second_peers(n):
         return columns if along_row(n) else [across]
 
@@ -64,7 +68,7 @@
     peers = [(me + d) % tiles for d in range(1, tiles)]
 
     barrier = pltpu.get_barrier_semaphore()
-    greeted = [{"tile": z} for z in peers] + [{"pop": q} for q in [partner, across] + columns]
+    greeted = [{"tile": z} for z in peers] + [{"pop": q} for q in [partner, across] + columns + [flipped(q) for q in [across] + columns]]
     for there in greeted:
         pl.semaphore_signal(barrier, inc=1, device_id=there, device_id_type=pl.DeviceIdType.MESH)
 
@@ -121,6 +125,9 @@
         t = steps - 1 - n
         for j, q in enumerate(first_peers(n)):
             sent.append(remote(history.at[t], near.at[j, t], near_send.at[j, n], near_recv.at[j, n], {"pop": q}))
+            if n in BOTH:
+                sent.append(remote(history.at[t], near_relay.at[j, t], relay_send.at[j, n], relay_recv.at[j, n],
+                                   {"pop": flipped(q)}))
         sent.append(remote(history.at[t], near_other.at[t], other_send.at[n], other_recv.at[n], {"pop": partner}))
     spread(value_out, start_value, start_send.at[0], start_recv.at[0])
     spread(mass_out, start_mass, start_send.at[1], start_recv.at[1])
@@ -143,6 +150,8 @@
         t = steps - 1 - n
         for j in range(len(first_peers(n))):
             arrived(near.at[j, t], near_recv.at[j, n])
+            if n in BOTH:
+                continue
             sent.append(remote(near.at[j, t], near_relay.at[j, t], relay_send.at[j, n], relay_recv.at[j, n],
                                {"pop": partner}))
 
@@ -308,6 +317,14 @@
         mass = mass + time_step * ((net_r - behind_r(net_r)) + net_c)
     mass_main[...] = mass[:, :width].reshape(tiles, rows, width)
     send_back(mass_main, density_out, 0)
+    wait_spread(start_value, start_send.at[0])
+    wait_spread(start_mass, start_send.at[1])
+    for g in range(steps // WINDOWS):
+        wait_spread(rim_in.at[g], rim_send.at[g])
+    for n in range(steps):
+        wait_spread(cost_in.at[n], cost_send.at[n])
+    for copy in sent:
+        copy.wait_send()
     for _, k, n in plan[last:]:
         stages[k][1](n)
 
@@ -317,15 +334,8 @@
     for t in reversed(range(steps)):
         values[t] = values[t] - grand[t:t + 1, :]
     wait_back(mass_main, density_out, 0)
-    wait_spread(start_value, start_send.at[0])
-    wait_spread(start_mass, start_send.at[1])
-    for g in range(steps // WINDOWS):
-        wait_spread(rim_in.at[g], rim_send.at[g])
     for n in range(steps):
-        wait_spread(cost_in.at[n], cost_send.at[n])
         wait_spread(edge_in.at[n], edge_send.at[n])
-    for copy in sent:
-        copy.wait_send()
 
 
 def finish(values, density, values_out, density_out, sems):

time: 29.9 us -> 29.8 us (level)
  no operation moved by 1% of the time
where the time goes in v5:
time: 29.8 us; the launch traced here: 29.7 us
  Pallas kernels  29 us (97%)
  between operations  0.64 us (2%)
    pallas_call x1, Pallas kernels, per_device(): pl.pallas_call(functools.partial(kernel, pops, tiles), out_shape=(pltpu.V...  28.2 us
    pallas_call x1, Pallas kernels, per_device(): pl.pallas_call(finish, out_shape=(jax.ShapeDtypeStruct((steps, rows, cols...  0.82 us

profile of v5, /device:TPU:0, one launch (start us, length us, event | category | flops | bytes accessed | tf_op | source)
XLA Modules:
  0.0 29.7 jit_solution(10771299931402841042)
XLA Ops:
  0.6 28.2 %shard_map.59 = (f32[8,8,2048]{2,1,0:T(8,128)S(1)}, f32[8,2048]{1,0:T(8,128)S(1)}) custom-call(s32[8,8]{1,0:T(8,128)} %weights_in.1, f32[8,2048]{1,0:T(8,128)} %bitcast.6, bf16[8,8,2048]{2,1,0:T(8,128)(2,1)} %bitcast.5, f32[8,2048]{1,0:T(8,128)} %bitcast.7), custom_call_target="tpu_custom_call" | custom-call | tf_op jit(solution)/shard_map/pallas_call | solution.py:363
  28.9 0.8 %shard_map.60 = (f32[8,8,2048]{2,1,0:T(8,128)}, f32[8,2048]{1,0:T(8,128)}) custom-call(f32[8,8,2048]{2,1,0:T(8,128)S(1)} %get-tuple-element.6.values, f32[8,2048]{1,0:T(8,128)S(1)} %get-tuple-element.7.density), custom_call_target="tpu_custom_call" | custom-call | tf_op jit(solution)/shard_map/pallas_call | solution.py:410

commit v6 on v5

--- a/solution.py
+++ b/solution.py
@@ -65,7 +65,8 @@
         far = [(line, 1 - plane)] if along_row(n) else [(a, plane) for a in behind]
         return [own, partner] + [pop_of(a, b, core) for a, b in far] + [pop_of(a, b, 1 - core) for a, b in far]
 
-    peers = [(me + d) % tiles for d in range(1, tiles)]
+    lower = 1 - me // (tiles // 2)
+    peers = [(me + d + lower * (tiles - 2 * d)) % tiles for d in range(1, tiles)]
 
     barrier = pltpu.get_barrier_semaphore()
     greeted = [{"tile": z} for z in peers] + [{"pop": q} for q in [partner, across] + columns + [flipped(q) for q in [across] + columns]]

time: 29.8 us -> 29.8 us (level)
  no operation moved by 1% of the time
where the time goes in v6:
time: 29.8 us; the launch traced here: 29.6 us
  Pallas kernels  29 us (97%)
  between operations  0.64 us (2%)
    pallas_call x1, Pallas kernels, per_device(): pl.pallas_call(functools.partial(kernel, pops, tiles), out_shape=(pltpu.V...  28.2 us
    pallas_call x1, Pallas kernels, per_device(): pl.pallas_call(finish, out_shape=(jax.ShapeDtypeStruct((steps, rows, cols...  0.82 us

profile of v6, /device:TPU:0, one launch (start us, length us, event | category | flops | bytes accessed | tf_op | source)
XLA Modules:
  0.0 29.6 jit_solution(1133209785982467457)
XLA Ops:
  0.6 28.2 %shard_map.59 = (f32[8,8,2048]{2,1,0:T(8,128)S(1)}, f32[8,2048]{1,0:T(8,128)S(1)}) custom-call(s32[8,8]{1,0:T(8,128)} %weights_in.1, f32[8,2048]{1,0:T(8,128)} %bitcast.6, bf16[8,8,2048]{2,1,0:T(8,128)(2,1)} %bitcast.5, f32[8,2048]{1,0:T(8,128)} %bitcast.7), custom_call_target="tpu_custom_call" | custom-call | tf_op jit(solution)/shard_map/pallas_call | solution.py:364
  28.8 0.8 %shard_map.60 = (f32[8,8,2048]{2,1,0:T(8,128)}, f32[8,2048]{1,0:T(8,128)}) custom-call(f32[8,8,2048]{2,1,0:T(8,128)S(1)} %get-tuple-element.6.values, f32[8,2048]{1,0:T(8,128)S(1)} %get-tuple-element.7.density), custom_call_target="tpu_custom_call" | custom-call | tf_op jit(solution)/shard_map/pallas_call | solution.py:411
